TPU v7x, 32 devices: a whole 2x2x4 slice. The times are simulated.
32 devices in a mesh: dp: 8 (over y, x, core), tp: 4 (over z).
Axes of the slice: x: 2, y: 2, z: 4, core: 2. Of those that a mesh axis runs over, the one named last changes fastest.
Arguments:
- tokens: bfloat16 [128, 8192], P('tp', 'dp'), may hold values from -6 to 6
- targets: bfloat16 [128, 8192], P('tp', 'dp'), may hold values from -6 to 6
- gate_weight: bfloat16 [8192, 16384], P('dp', 'tp'), may hold values from -0.0625 to 0.0625
- up_weight: bfloat16 [8192, 16384], P('dp', 'tp'), may hold values from -0.0625 to 0.0625
- down_weight: bfloat16 [16384, 8192], P('tp', 'dp'), may hold values from -0.046875 to 0.046875
- direction_gate: bfloat16 [8192, 16384], P('dp', 'tp'), may hold values from -36 to 36
- direction_up: bfloat16 [8192, 16384], P('dp', 'tp'), may hold values from -36 to 36
- direction_down: bfloat16 [16384, 8192], P('tp', 'dp'), may hold values from -36 to 36
- previous_gate: bfloat16 [8192, 16384], P('dp', 'tp'), may hold values from -36 to 36
- previous_up: bfloat16 [8192, 16384], P('dp', 'tp'), may hold values from -36 to 36
- previous_down: bfloat16 [16384, 8192], P('tp', 'dp'), may hold values from -36 to 36
- beta_prev: float32 [1], replicated, may hold values from 1 to 4
Outputs:
- next_gate: bfloat16 [8192, 16384], P('dp', 'tp')
- next_up: bfloat16 [8192, 16384], P('dp', 'tp')
- next_down: bfloat16 [16384, 8192], P('tp', 'dp')
- coefficients: float32 [2], replicated
All inputs are finite; a program needn't handle non-finite values.
Results may differ from a plain program's by a relative error of at most 0.015.
Values may be sent and summed in bfloat16 or wider, within the bound.
A program may use at most 256 MiB of HBM per device.

v0:
```python
import jax
import jax.numpy as jnp
from jax import lax
from jax.sharding import PartitionSpec as P

D = 8192
FF = 16384


def product(first_op, second_op):
    return jnp.dot(first_op, second_op, preferred_element_type=jnp.float32)


def against(first_op, second_op):
    return lax.dot_general(
        first_op, second_op, (((1,), (1,)), ((), ())), preferred_element_type=jnp.float32
    )


def transposed(first_op, second_op):
    return lax.dot_general(
        first_op, second_op, (((0,), (0,)), ((), ())), preferred_element_type=jnp.float32
    )


def pointwise(gate_sum):
    logistic = jax.nn.sigmoid(gate_sum)
    activation = gate_sum * logistic
    gate_slope = logistic * (1.0 + gate_sum * (1.0 - logistic))
    gate_curve = logistic * (1.0 - logistic) * (2.0 + gate_sum * (1.0 - 2.0 * logistic))
    return (activation, gate_slope, gate_curve)


def forward_share(gate_sum, up_sum, gate_dir, up_dir):
    activation, gate_slope, gate_curve = pointwise(gate_sum)
    hidden = (activation * up_sum).astype(jnp.bfloat16)
    hidden_dir = (gate_slope * up_sum * gate_dir + activation * up_dir).astype(jnp.bfloat16)
    return (hidden, hidden_dir, activation, gate_slope, gate_curve)


def backward_share(
    grad_hidden, grad_hidden_dir, up_sum, gate_dir, up_dir, activation, gate_slope, gate_curve
):
    grad_gate_dir = (
        grad_hidden_dir * up_sum * gate_slope
        + grad_hidden * up_dir * gate_slope
        + grad_hidden * up_sum * gate_curve * gate_dir
    ).astype(jnp.bfloat16)
    grad_up_dir = (grad_hidden_dir * activation + grad_hidden * gate_slope * gate_dir).astype(
        jnp.bfloat16
    )
    return (grad_gate_dir, grad_up_dir)


def inner_sum(first_list, second_list):
    return sum(
        (
            jnp.sum(first_part * second_part)
            for first_part, second_part in zip(first_list, second_list)
        )
    )


def on_device(
    tokens,
    targets,
    gate_weight,
    up_weight,
    down_weight,
    direction_gate,
    direction_up,
    direction_down,
    previous_gate,
    previous_up,
    previous_down,
    beta_prev,
):
    width_part = gate_weight.shape[1]
    model_part = down_weight.shape[1]
    everyone = lax.all_gather(tokens, "tp", axis=0, tiled=True)
    total_rows = everyone.shape[0]
    front = lax.psum_scatter(
        jnp.concatenate(
            [
                product(everyone, gate_weight),
                product(everyone, up_weight),
                product(everyone, direction_gate),
                product(everyone, direction_up),
            ],
            axis=1,
        ),
        "dp",
        scatter_dimension=0,
        tiled=True,
    )
    gate_sum = front[:, :width_part]
    up_sum = front[:, width_part : 2 * width_part]
    gate_dir = front[:, 2 * width_part : 3 * width_part]
    up_dir = front[:, 3 * width_part :]
    hidden, hidden_dir, activation, gate_slope, gate_curve = forward_share(
        gate_sum, up_sum, gate_dir, up_dir
    )
    hidden_all, hidden_dir_all = (
        lax.all_gather(hidden, "dp", axis=0, tiled=True),
        lax.all_gather(hidden_dir, "dp", axis=0, tiled=True),
    )
    sums = lax.psum_scatter(
        jnp.concatenate(
            [
                product(hidden_all, down_weight),
                product(hidden_dir_all, down_weight) + product(hidden_all, direction_down),
            ],
            axis=1,
        ),
        "tp",
        scatter_dimension=0,
        tiled=True,
    )
    grad_out = ((sums[:, :model_part] - targets.astype(jnp.float32)) / total_rows).astype(
        jnp.bfloat16
    )
    grad_out_dir = (sums[:, model_part:] / total_rows).astype(jnp.bfloat16)
    grad_out_all, grad_out_dir_all = (
        lax.all_gather(grad_out, "tp", axis=0, tiled=True),
        lax.all_gather(grad_out_dir, "tp", axis=0, tiled=True),
    )
    grads = lax.psum_scatter(
        jnp.concatenate(
            [
                against(grad_out_all, down_weight),
                against(grad_out_dir_all, down_weight) + against(grad_out_all, direction_down),
            ],
            axis=1,
        ).astype(jnp.bfloat16),
        "dp",
        scatter_dimension=0,
        tiled=True,
    ).astype(jnp.float32)
    grad_gate_dir, grad_up_dir = backward_share(
        grads[:, :width_part],
        grads[:, width_part:],
        up_sum,
        gate_dir,
        up_dir,
        activation,
        gate_slope,
        gate_curve,
    )
    gate_dir_all, up_dir_all = (
        lax.all_gather(grad_gate_dir, "dp", axis=0, tiled=True),
        lax.all_gather(grad_up_dir, "dp", axis=0, tiled=True),
    )
    image_gate = transposed(everyone, gate_dir_all)
    image_up = transposed(everyone, up_dir_all)
    image_down = transposed(hidden_dir_all, grad_out_all) + transposed(hidden_all, grad_out_dir_all)
    images = [image_gate, image_up, image_down]
    alongs = [
        matrix.astype(jnp.float32) for matrix in (direction_gate, direction_up, direction_down)
    ]
    befores = [matrix.astype(jnp.float32) for matrix in (previous_gate, previous_up, previous_down)]
    entries = 3 * D * FF
    beta_old = beta_prev[0]
    totals = lax.psum(
        (
            inner_sum(images, images),
            inner_sum(images, alongs),
            inner_sum(images, befores),
            inner_sum(alongs, alongs),
            inner_sum(alongs, befores),
            inner_sum(befores, befores),
        ),
        ("dp", "tp"),
    )
    image_image, image_along, image_before, along_along, along_before, before_before = totals
    alpha_coef = image_along / entries
    square = (
        image_image
        - 2.0 * alpha_coef * image_along
        - 2.0 * beta_old * image_before
        + alpha_coef * alpha_coef * along_along
        + 2.0 * alpha_coef * beta_old * along_before
        + beta_old * beta_old * before_before
    )
    beta_coef = jnp.sqrt(square / entries + 1e-06)
    residuals = [
        image_part - alpha_coef * along_part - beta_old * before_part
        for image_part, along_part, before_part in zip(images, alongs, befores)
    ]
    next_parts = [(matrix / beta_coef).astype(jnp.bfloat16) for matrix in residuals]
    return (next_parts[0], next_parts[1], next_parts[2], jnp.stack([alpha_coef, beta_coef]))


def solution(mesh):
    in_specs = (
        P("tp", "dp"),
        P("tp", "dp"),
        P("dp", "tp"),
        P("dp", "tp"),
        P("tp", "dp"),
        P("dp", "tp"),
        P("dp", "tp"),
        P("tp", "dp"),
        P("dp", "tp"),
        P("dp", "tp"),
        P("tp", "dp"),
        P(),
    )
    out_specs = (P("dp", "tp"), P("dp", "tp"), P("tp", "dp"), P())
    return jax.shard_map(
        on_device, mesh=mesh, in_specs=in_specs, out_specs=out_specs, check_vma=False
    )
```

profile of v0, /device:TPU:0, one launch (start us, length us, event | category | flops | bytes accessed | tf_op | source)
XLA Modules:
  0.0 505.3 jit_solution(11897360157032648678)
XLA Ops:
  7.2 16.0 %all_gather.21 = bf16[128,1024]{1,0:T(8,128)(2,1)S(1)} all-gather(bf16[32,1024]{1,0:T(8,128)(2,1)} %param.12), channel_id=1, replica_groups=mesh['dp'=8,'tp'=4] {'tp'}, dimensions={0}, use_global_device_ids=true | all-gather | bytes 327680 | tf_op jit(solution)/shard_map/all_gather | solution.py:80
  23.2 4.8 fusion.44
  29.4 2.1 copy-done
  35.4 3.7 pad_maximum_fusion
  39.2 73.1 %reduce-scatter.4.cloned.1.call-done = f32[16,16384]{1,0:T(8,128)} async-done(((f32[128,16384]{1,0:T(8,128)}), f32[16,16384]{1,0:T(8,128)}) %reduce-scatter.4.cloned.1.call-update) | async-done | bytes 1048592 | tf_op jit(solution)/shard_map/reduce_scatter | solution.py:82
  112.3 2.0 multiply_convert_fusion
  115.1 23.0 %all-gather.7.cloned.1.call-done = bf16[128,4096]{1,0:T(8,128)(2,1)} async-done(((bf16[16,4096]{1,0:T(8,128)(2,1)}), bf16[128,4096]{1,0:T(8,128)(2,1)}) %all-gather.7.cloned.1.call-update) | async-done | bytes 1048592 | tf_op jit(solution)/shard_map/all_gather | solution.py:105
  138.1 5.0 fusion.46
  143.1 20.9 %all-gather.5.cloned.1.call-done = bf16[128,4096]{1,0:T(8,128)(2,1)} async-done(((bf16[16,4096]{1,0:T(8,128)(2,1)}), bf16[128,4096]{1,0:T(8,128)(2,1)}) %all-gather.5.cloned.1.call-update) | async-done | bytes 1048592 | tf_op jit(solution)/shard_map/all_gather | solution.py:104
  164.0 5.0 fusion.45
  169.1 4.7 convolution_add_fusion.2
  174.9 27.4 %reduce-scatter.6.cloned.1.call-done = f32[32,2048]{1,0:T(8,128)} async-done(((f32[128,2048]{1,0:T(8,128)}), f32[32,2048]{1,0:T(8,128)}) %reduce-scatter.6.cloned.1.call-update) | async-done | bytes 262160 | tf_op jit(solution)/shard_map/reduce_scatter | solution.py:107
  203.3 14.3 %all_gather.24 = bf16[128,1024]{1,0:T(8,128)(2,1)S(1)} all-gather(bf16[32,1024]{1,0:T(8,128)(2,1)S(1)} %get-tuple-element.36), channel_id=1, replica_groups=mesh['dp'=8,'tp'=4] {'tp'}, dimensions={0}, use_global_device_ids=true | all-gather | bytes 327680 | tf_op jit(solution)/shard_map/all_gather | solution.py:124
  217.5 14.0 %all_gather.25 = bf16[128,1024]{1,0:T(8,128)(2,1)S(1)} all-gather(bf16[32,1024]{1,0:T(8,128)(2,1)S(1)} %get-tuple-element.37), channel_id=1, replica_groups=mesh['dp'=8,'tp'=4] {'tp'}, dimensions={0}, use_global_device_ids=true | all-gather | bytes 327680 | tf_op jit(solution)/shard_map/all_gather | solution.py:125
  231.6 6.4 %convolution_convert_fusion = bf16[128,4096]{1,0:T(8,128)(2,1)S(1)} fusion(bf16[128,1024]{1,0:T(8,128)(2,1)S(1)} %all_gather.24, bf16[4096,1024]{1,0:T(8,128)(2,1)} %param.16), kind=kOutput, calls=%fused_computation.57 | convolution fusion | flops 1074266112 | bytes 9699328 | tf_op jit(solution)/shard_map/dot_general | solution.py:15
  238.0 6.4 %fusion.47 = f32[128,4096]{1,0:T(8,128)S(1)} fusion(bf16[128,1024]{1,0:T(8,128)(2,1)S(1)} %all_gather.25, bf16[4096,1024]{1,0:T(8,128)(2,1)} %param.16), kind=kOutput, calls=%fused_computation.87 | convolution fusion | flops 1073741824 | bytes 10747904 | tf_op jit(solution)/shard_map/dot_general | solution.py:15
  244.4 2.8 fusion.29
  248.8 12.1 %copy.16 = bf16[1024,4096]{0,1:T(8,128)(2,1)} copy(bf16[1024,4096]{1,0:T(8,128)(2,1)} %param.17) | data formatting | bytes 16777216 | tf_op args[5]
  261.0 11.9 %copy.17 = bf16[1024,4096]{0,1:T(8,128)(2,1)} copy(bf16[1024,4096]{1,0:T(8,128)(2,1)} %param.18) | data formatting | bytes 16777216 | tf_op args[6]
  273.5 12.0 %copy.18 = bf16[1024,4096]{0,1:T(8,128)(2,1)} copy(bf16[1024,4096]{1,0:T(8,128)(2,1)} %param.20) | data formatting | bytes 16777216 | tf_op args[8]
  285.5 12.0 %copy.19 = bf16[1024,4096]{0,1:T(8,128)(2,1)} copy(bf16[1024,4096]{1,0:T(8,128)(2,1)} %param.21) | data formatting | bytes 16777216 | tf_op args[9]
  297.5 8.1 %fusion.48 = f32[4096,1024]{1,0:T(8,128)} fusion(bf16[128,4096]{1,0:T(8,128)(2,1)S(1)} %copy-done.2, bf16[128,1024]{1,0:T(8,128)(2,1)S(1)} %all_gather.24), kind=kOutput, calls=%fused_computation.88 | convolution fusion | flops 1073741824 | bytes 18087936 | tf_op jit(solution)/shard_map/dot_general | solution.py:21
  306.5 2.1 add_convert_fusion
  309.0 20.1 %fusion.21 = (f32[]{:T(128)}, f32[]{:T(128)}, f32[]{:T(128)}, f32[]{:T(128)}, f32[]{:T(128)}, /*index=5*/f32[]{:T(128)}, f32[4096,1024]{1,0:T(8,128)}) fusion(bf16[4096,1024]{1,0:T(8,128)(2,1)} %param.22, bf16[4096,1024]{1,0:T(8,128)(2,1)} %param.19, f32[4096,1024]{1,0:T(8,128)} %fusion.48, bf16[128,4096]{1,0:T(8,128)(2,1)S(1)} %copy-done.1, ...), kind=kOutput, calls=%fused_computation.42 | convolution fusion | flops 1136656384 | bytes 51642392 | tf_op jit(solution)/shard_map/dot_general | solution.py:21
  330.6 16.9 %fusion.18 = (f32[]{:T(128)}, f32[]{:T(128)}, f32[]{:T(128)}, f32[]{:T(128)}, f32[]{:T(128)}, /*index=5*/f32[]{:T(128)}, f32[4096,1024]{1,0:T(8,128)}) fusion(bf16[1024,4096]{0,1:T(8,128)(2,1)} %copy.19, bf16[1024,4096]{0,1:T(8,128)(2,1)} %copy.17, bf16[128,4096]{1,0:T(8,128)(2,1)} %all-gather.11.cloned.1.call-done, bf16[128,1024]{1,0:T(8,128)(2,1)S(1)} %all_gather.21), kind=kOutput, calls=%fused_computation.39 | convolution fusion | flops 1132462080 | bytes 34865176 | tf_op jit(solution)/shard_map/dot_general | solution.py:21
  347.5 8.4 %all-gather.9.cloned.1.call-done = bf16[128,4096]{1,0:T(8,128)(2,1)} async-done(((bf16[16,4096]{1,0:T(8,128)(2,1)}), bf16[128,4096]{1,0:T(8,128)(2,1)}) %all-gather.9.cloned.1.call-update) | async-done | bytes 1048592 | tf_op jit(solution)/shard_map/all_gather | solution.py:150
  355.9 16.9 %fusion.15 = (f32[]{:T(128)}, f32[]{:T(128)}, f32[]{:T(128)}, f32[]{:T(128)}, f32[]{:T(128)}, /*index=5*/f32[]{:T(128)}, f32[4096,1024]{1,0:T(8,128)}) fusion(bf16[1024,4096]{0,1:T(8,128)(2,1)} %copy.18, bf16[1024,4096]{0,1:T(8,128)(2,1)} %copy.16, bf16[128,4096]{1,0:T(8,128)(2,1)} %all-gather.9.cloned.1.call-done, bf16[128,1024]{1,0:T(8,128)(2,1)S(1)} %all_gather.21), kind=kOutput, calls=%fused_computation.36 | convolution fusion | flops 1132462080 | bytes 34865176 | tf_op jit(solution)/shard_map/dot_general | solution.py:21
  384.1 39.6 %all-reduce = (f32[]{:T(128)}, f32[]{:T(128)}, f32[]{:T(128)}, f32[]{:T(128)}, f32[]{:T(128)}, /*index=5*/f32[]{:T(128)}) all-reduce(f32[]{:T(128)S(6)} %add.109, f32[]{:T(128)S(6)} %add.107, f32[]{:T(128)S(6)} %add.111, f32[]{:T(128)S(6)} %add.113, f32[]{:T(128)S(6)} %add.116, f32[]{:T(128)S(6)} %add.119), channel_id=1, replica_groups=mesh['dp'=8,'tp'=4] {'dp','tp'}, use_global_device_ids=true, to_apply=%region_10.0 | all-reduce | flops 6 | bytes 48 | tf_op jit(solution)/shard_map/psum | solution.py:163
  429.7 29.5 %fusion.27 = (bf16[1024,4096]{0,1:T(8,128)(2,1)}, bf16[1024,4096]{0,1:T(8,128)(2,1)}) fusion(bf16[1024,4096]{0,1:T(8,128)(2,1)} %copy.19, bf16[1024,4096]{0,1:T(8,128)(2,1)} %copy.17, f32[4096,1024]{1,0:T(8,128)} %get-tuple-element.39, f32[]{:T(128)} %sqrt.3, f32[]{:T(128)} %bitcast.49, f32[]{:T(128)} %div.34, bf16[1024,4096]{0,1:T(8,128)(2,1)} %copy.18, ...), kind=kLoop, calls=%fused_computation.51 | loop fusion | flops 67108864 | bytes 83886096 | tf_op jit(solution)/shard_map/convert_element_type | solution.py:189
  459.2 11.9 %copy.21 = bf16[1024,4096]{1,0:T(8,128)(2,1)} copy(bf16[1024,4096]{0,1:T(8,128)(2,1)} %get-tuple-element.41) | data formatting | bytes 16777216
  471.1 11.9 %copy.20 = bf16[1024,4096]{1,0:T(8,128)(2,1)} copy(bf16[1024,4096]{0,1:T(8,128)(2,1)} %get-tuple-element.42) | data formatting | bytes 16777216
  483.0 14.9 %fusion.26 = bf16[4096,1024]{1,0:T(8,128)(2,1)} fusion(bf16[4096,1024]{1,0:T(8,128)(2,1)} %param.22, f32[4096,1024]{1,0:T(8,128)} %get-tuple-element.40, bf16[4096,1024]{1,0:T(8,128)(2,1)} %param.19, f32[]{:T(128)} %sqrt.3, f32[]{:T(128)} %bitcast.54, f32[]{:T(128)} %div.34), kind=kLoop, calls=%fused_computation.50 | loop fusion | flops 33554432 | bytes 41943052 | tf_op jit(solution)/shard_map/convert_element_type | solution.py:189
  (46 shorter events, 13.2 us)
Async XLA Ops:
  7.2 105.1 %reduce-scatter.4.cloned.1.call-start = ((), (), s32[]{:S(2)}) async-start(), calls=%async_computation.3 | async-start | bytes 9437184 | tf_op jit(solution)/shard_map/reduce_scatter | solution.py:82
  7.2 20.8 %slice-start.2 = ((s8[8388608]{0:T(1024)(128)(4,1)}), s8[4194304]{0:T(1024)(128)(4,1)S(1)}, s32[]{:S(2)}) async-start(s8[8388608]{0:T(1024)(128)(4,1)} %bitcast.57), calls=%async_computation.12 | async-start | bytes 8388608
  23.2 4.8 slice-start.3
  28.1 3.4 copy-start
  28.1 4.7 slice-start.4
  31.4 2.6 slice-start.5
  39.1 99.0 %all-gather.7.cloned.1.call-start = ((), (), s32[]{:S(2)}) async-start(), calls=%async_computation.5 | async-start | bytes 1179648 | tf_op jit(solution)/shard_map/all_gather | solution.py:105
  114.3 49.7 %all-gather.5.cloned.1.call-start = ((), (), s32[]{:S(2)}) async-start(), calls=%async_computation.4 | async-start | bytes 1179648 | tf_op jit(solution)/shard_map/all_gather | solution.py:104
  115.1 87.2 %reduce-scatter.6.cloned.1.call-start = ((), (), s32[]{:S(2)}) async-start(), calls=%async_computation.6 | async-start | bytes 1310720 | tf_op jit(solution)/shard_map/reduce_scatter | solution.py:107
  164.0 5.0 copy-start.1
  169.1 33.2 %copy-start.3 = (bf16[32,1024]{1,0:T(8,128)(2,1)S(1)}, bf16[32,1024]{1,0:T(8,128)(2,1)}, u32[]{:S(2)}) copy-start(bf16[32,1024]{1,0:T(8,128)(2,1)} %param.13) | copy-start | bytes 196612
  174.8 130.7 %reduce-scatter.8.cloned.1.call-start = ((), (), s32[]{:S(2)}) async-start(), calls=%async_computation.7 | async-start | bytes 2359296 | tf_op jit(solution)/shard_map/reduce_scatter | solution.py:127
  231.6 12.8 %slice-start = ((s8[8388608]{0:T(1024)(128)(4,1)}), s8[4194304]{0:T(1024)(128)(4,1)S(1)}, s32[]{:S(2)}) async-start(s8[8388608]{0:T(1024)(128)(4,1)} %bitcast.55), calls=%async_computation.10 | async-start | bytes 8388608
  238.0 6.4 %slice-start.1 = ((s8[8388608]{0:T(1024)(128)(4,1)}), s8[4194304]{0:T(1024)(128)(4,1)S(1)}, s32[]{:S(2)}) async-start(s8[8388608]{0:T(1024)(128)(4,1)} %bitcast.55), calls=%async_computation.11 | async-start | bytes 8388608
  248.8 81.8 %all-gather.11.cloned.1.call-start = ((), (), s32[]{:S(2)}) async-start(), calls=%async_computation.9 | async-start | bytes 1179648 | tf_op jit(solution)/shard_map/all_gather | solution.py:151
  285.5 12.0 %copy-start.2 = (bf16[128,4096]{1,0:T(8,128)(2,1)S(1)}, bf16[128,4096]{1,0:T(8,128)(2,1)}, u32[]{:S(2)}) copy-start(bf16[128,4096]{1,0:T(8,128)(2,1)} %all-gather.7.cloned.1.call-done) | copy-start | bytes 3145732
  308.7 47.2 %all-gather.9.cloned.1.call-start = ((), (), s32[]{:S(2)}) async-start(), calls=%async_computation.8 | async-start | bytes 1179648 | tf_op jit(solution)/shard_map/all_gather | solution.py:150
Sparse Core Ops, SparseCore 0:
  39.2 73.0 reduce-scatter.3
  114.7 23.3 all-gather.6
  140.6 23.3 all-gather.4
  174.9 27.2 reduce-scatter.5
  248.9 39.4 reduce-scatter.7
  308.8 21.7 all-gather.10
  332.5 23.3 all-gather.8
where the time goes:
time: 508 us; the launch traced here: 505 us
  waiting for transfers between devices  155 us (31%)
  matrix products  101 us (20%)
  blocking collectives  83.9 us (17%)
  local copies, waits for them, and re-layouts  75.3 us (15%)
  other arithmetic  57.3 us (11%)
  between operations  32.3 us (6%)
    unnamed x26, local copies, waits for them, and re-layouts  75.3 us
    reduce_scatter x1, waiting for transfers between devices, on_device(): lax.psum_scatter(jnp.concatenate([product(everyone, gate_weight), product...  73.1 us
    dot_general x4, matrix products, transposed(): lax.dot_general(first_op, second_op, (((0,), (0,)), ((), ())), preferred_...  62 us
    convert_element_type x2, other arithmetic, on_device(): (matrix / beta_coef).astype(jnp.bfloat16)  44.4 us
    psum x1, blocking collectives, on_device(): lax.psum((inner_sum(images, images), inner_sum(images, alongs), inner_sum...  39.6 us
    reduce_scatter x1, waiting for transfers between devices, on_device(): lax.psum_scatter(jnp.concatenate([product(hidden_all, down_weight), produ...  27.4 us
    dot_general x7, matrix products, product(): return jnp.dot(first_op, second_op, preferred_element_type=jnp.float32)  23.3 us
    all_gather x1, waiting for transfers between devices, on_device(): lax.all_gather(hidden_dir, 'dp', axis=0, tiled=True)  23 us
  transfers between devices with their start and end apart: 7, of which 6 were waited for; matrix products, arithmetic and copies ran while one was open for 19% of the time, Pallas kernels for 0%

commit v1 on v0

v1 whole, which is shorter than its diff:
```python
import functools

import jax
import jax.numpy as jnp
from jax import lax
from jax.experimental import pallas as pl
from jax.experimental.pallas import tpu as pltpu
from jax.sharding import PartitionSpec as P

MESH = pl.DeviceIdType.MESH
VMEM = pltpu.VMEM
DMA = pltpu.SemaphoreType.DMA
F32 = jnp.float32
BF16 = jnp.bfloat16
LIMIT = 56 * 1024 * 1024


def tile_of(size, most):
    tile = min(size, most)
    while size % tile:
        tile //= 2
    return tile


def greet(targets):
    barrier = pltpu.get_barrier_semaphore()
    for target in targets:
        pl.semaphore_signal(barrier, inc=1, device_id=target, device_id_type=MESH)
    pl.semaphore_wait(barrier, len(targets))


def send(src, dst, send_sem, recv_sem, target):
    copy = pltpu.make_async_remote_copy(
        src_ref=src, dst_ref=dst, send_sem=send_sem, recv_sem=recv_sem, device_id=target, device_id_type=MESH
    )
    copy.start()
    return copy


def by_columns(width, body):
    step = tile_of(width, 512)

    @pl.loop(0, width // step)
    def _(i):
        body(pl.ds(pl.multiple_of(i * step, step), step))


def forward_rows(parts, keeps, cols):
    gate_sum, up_sum, gate_dir, up_dir = parts
    for keep, part in zip(keeps, parts):
        keep[:, cols] = part
    logistic = jax.nn.sigmoid(gate_sum)
    activation = gate_sum * logistic
    gate_slope = logistic * (1.0 + gate_sum * (1.0 - logistic))
    hidden = activation * up_sum
    hidden_dir = gate_slope * up_sum * gate_dir + activation * up_dir
    return hidden, hidden_dir


def backward_rows(parts, keeps, cols):
    grad_hidden, grad_hidden_dir = parts
    gate_sum, up_sum, gate_dir, up_dir = (keep[:, cols] for keep in keeps)
    logistic = jax.nn.sigmoid(gate_sum)
    activation = gate_sum * logistic
    gate_slope = logistic * (1.0 + gate_sum * (1.0 - logistic))
    gate_curve = logistic * (1.0 - logistic) * (2.0 + gate_sum * (1.0 - 2.0 * logistic))
    grad_gate = (
        grad_hidden_dir * up_sum * gate_slope
        + grad_hidden * up_dir * gate_slope
        + grad_hidden * up_sum * gate_curve * gate_dir
    )
    grad_up = grad_hidden_dir * activation + grad_hidden * gate_slope * gate_dir
    return grad_gate, grad_up


def width_kernel(n, kinds, rows_of, keeps_in, *refs):
    x = refs[0]
    if keeps_in:
        keeps, out = refs[1:5], refs[5]
    else:
        out, keeps = refs[1], refs[2:6]
    mate_in, paired, far_in, full, s1, r1, s2, r2, s3, r3, s4, r4, local = refs[6:]
    chips = n // 2
    width = x.shape[-1]
    me = lax.axis_index("dp")
    chip, core = lax.div(me, 2), lax.rem(me, 2)
    mate = {"dp": me + 1 - 2 * core}
    afar = [{"dp": lax.rem(chip + s, chips) * 2 + core} for s in range(1, chips)]
    greet([mate] + afar)

    order = list(range(1, chips)) + [0]
    spot = [lax.rem(chip + s, chips) for s in range(chips)]
    source = [lax.rem(chip + chips - s, chips) for s in range(chips)]
    first = {
        s: send(x.at[:, spot[s], 1 - core], mate_in.at[:, spot[s]], s1.at[s], r1.at[s], mate)
        for s in order
    }
    second = {}
    for s in order:
        first[s].wait_recv()

        def pair(cols, s=s):
            for kind in range(kinds):
                paired[kind, spot[s], :, cols] = (
                    x[kind, spot[s], core, :, cols].astype(F32)
                    + mate_in[kind, spot[s], :, cols].astype(F32)
                ).astype(BF16)

        by_columns(width, pair)
        if s:
            second[s] = send(
                paired.at[:, spot[s]], far_in.at[:, chip], s2.at[s], r2.at[s], afar[s - 1]
            )
    for s in range(1, chips):
        second[s].wait_recv()

    def finish(cols):
        parts = []
        for kind in range(kinds):
            total = paired[kind, chip, :, cols].astype(F32)
            for s in range(1, chips):
                total = total + far_in[kind, source[s], :, cols].astype(F32)
            parts.append(total)
        one, two = rows_of(parts, keeps, cols)
        full[0, me, :, cols] = one.astype(BF16)
        full[1, me, :, cols] = two.astype(BF16)

    by_columns(width, finish)

    mine = full.at[:, me]
    third = [send(mine, mine, s3.at[s], r3.at[s], afar[s - 1]) for s in range(1, chips)]
    fourth = [send(mine, mine, s4.at[0], r4.at[0], mate)]
    stores = [pltpu.make_async_copy(mine, out.at[:, me], local.at[0])]
    stores[0].start()
    for s in range(1, chips):
        third[s - 1].wait_recv()
        at = source[s] * 2 + core
        fourth.append(send(full.at[:, at], full.at[:, at], s4.at[s], r4.at[s], mate))
        store = pltpu.make_async_copy(full.at[:, at], out.at[:, at], local.at[s])
        store.start()
        stores.append(store)
    for s in range(chips):
        fourth[s].wait_recv()
        at = source[s] * 2 + 1 - core
        store = pltpu.make_async_copy(full.at[:, at], out.at[:, at], local.at[chips + s])
        store.start()
        stores.append(store)
    for copy in list(first.values()) + list(second.values()) + third + fourth:
        copy.wait_send()
    for store in stores:
        store.wait()


def width_exchange(n, x, keeps, rows_of, collective_id):
    kinds, rows, width = x.shape
    share, chips = rows // n, n // 2
    keeps_in = keeps is not None
    x = x.reshape(kinds, chips, 2, share, width)
    vmem, anywhere = pl.BlockSpec(memory_space=VMEM), pl.BlockSpec(memory_space=pl.ANY)
    out_shape = [jax.ShapeDtypeStruct((2, n, share, width), BF16)]
    out_specs = [anywhere]
    if not keeps_in:
        out_shape += [jax.ShapeDtypeStruct((share, width), F32)] * 4
        out_specs += [vmem] * 4
    slots = VMEM((kinds, chips, share, width), BF16)
    sems = DMA((chips,))
    result = pl.pallas_call(
        functools.partial(width_kernel, n, kinds, rows_of, keeps_in),
        out_shape=out_shape,
        in_specs=[vmem] * (5 if keeps_in else 1),
        out_specs=out_specs,
        scratch_shapes=[slots, slots, slots, VMEM((2, n, share, width), BF16)]
        + [sems] * 8
        + [DMA((n,))],
        compiler_params=pltpu.CompilerParams(
            collective_id=collective_id, has_side_effects=True, vmem_limit_bytes=LIMIT
        ),
    )(x, *(keeps or ()))
    return result[0].reshape(2, rows, width), tuple(result[1:])


def ring_of(t):
    me = lax.axis_index("tp")
    return me, [lax.rem(me + s, t) for s in range(1, t)], [lax.rem(me + t - s, t) for s in range(1, t)]


def tokens_kernel(t, x, out, full, ssem, rsem, local):
    me, spots, sources = ring_of(t)
    greet([{"tp": spot} for spot in spots])
    copies = [
        send(x, full.at[me], ssem.at[i], rsem.at[i], {"tp": spot}) for i, spot in enumerate(spots)
    ]
    stores = [pltpu.make_async_copy(x, out.at[me], local.at[t - 1])]
    stores[0].start()
    for i, copy in enumerate(copies):
        copy.wait_recv()
        store = pltpu.make_async_copy(full.at[sources[i]], out.at[sources[i]], local.at[i])
        store.start()
        stores.append(store)
    for copy in copies:
        copy.wait_send()
    for store in stores:
        store.wait()


def tokens_exchange(t, x):
    share, width = x.shape
    out = pl.pallas_call(
        functools.partial(tokens_kernel, t),
        out_shape=jax.ShapeDtypeStruct((t, share, width), BF16),
        in_specs=[pl.BlockSpec(memory_space=VMEM)],
        out_specs=pl.BlockSpec(memory_space=pl.ANY),
        scratch_shapes=[VMEM((t, share, width), BF16), DMA((t - 1,)), DMA((t - 1,)), DMA((t,))],
        compiler_params=pltpu.CompilerParams(
            collective_id=1, has_side_effects=True, vmem_limit_bytes=LIMIT
        ),
    )(x)
    return out.reshape(t * share, width)


def output_kernel(t, x, targets, out, far_in, full, s1, r1, s2, r2, local):
    me, spots, sources = ring_of(t)
    share, width = targets.shape
    rows = t * share
    greet([{"tp": spot} for spot in spots])
    first = [
        send(x.at[:, spot], far_in.at[:, me], s1.at[i], r1.at[i], {"tp": spot})
        for i, spot in enumerate(spots)
    ]
    for copy in first:
        copy.wait_recv()

    def finish(cols):
        parts = []
        for kind in range(2):
            total = x[kind, me, :, cols].astype(F32)
            for at in sources:
                total = total + far_in[kind, at, :, cols].astype(F32)
            parts.append(total)
        full[0, me, :, cols] = ((parts[0] - targets[:, cols].astype(F32)) / rows).astype(BF16)
        full[1, me, :, cols] = (parts[1] / rows).astype(BF16)

    by_columns(width, finish)
    mine = full.at[:, me]
    second = [
        send(mine, mine, s2.at[i], r2.at[i], {"tp": spot}) for i, spot in enumerate(spots)
    ]
    stores = [pltpu.make_async_copy(mine, out.at[:, me], local.at[t - 1])]
    stores[0].start()
    for i, copy in enumerate(second):
        copy.wait_recv()
        at = sources[i]
        store = pltpu.make_async_copy(full.at[:, at], out.at[:, at], local.at[i])
        store.start()
        stores.append(store)
    for copy in first + second:
        copy.wait_send()
    for store in stores:
        store.wait()


def output_exchange(t, x, targets):
    _, rows, width = x.shape
    share = rows // t
    vmem = pl.BlockSpec(memory_space=VMEM)
    slots = VMEM((2, t, share, width), BF16)
    out = pl.pallas_call(
        functools.partial(output_kernel, t),
        out_shape=jax.ShapeDtypeStruct((2, t, share, width), BF16),
        in_specs=[vmem, vmem],
        out_specs=pl.BlockSpec(memory_space=pl.ANY),
        scratch_shapes=[slots, slots] + [DMA((t - 1,))] * 4 + [DMA((t,))],
        compiler_params=pltpu.CompilerParams(
            collective_id=2, has_side_effects=True, vmem_limit_bytes=LIMIT
        ),
    )(x.reshape(2, t, share, width), targets)
    return out.reshape(2, rows, width)


def totals_kernel(n, t, x, out, dp_in, sums, tp_in, s1, r1, s2, r2, local):
    dp, tp = lax.axis_index("dp"), lax.axis_index("tp")
    dp_spots = [lax.rem(dp + s, n) for s in range(1, n)]
    tp_spots = [lax.rem(tp + s, t) for s in range(1, t)]
    greet([{"dp": spot} for spot in dp_spots] + [{"tp": spot} for spot in tp_spots])
    first = [
        send(x, dp_in.at[dp], s1.at[i], r1.at[i], {"dp": spot}) for i, spot in enumerate(dp_spots)
    ]
    dp_in[dp] = x[...]
    for copy in first:
        copy.wait_recv()
    total = dp_in[0]
    for at in range(1, n):
        total = total + dp_in[at]
    sums[...] = total
    tp_in[tp] = total
    second = [
        send(sums, tp_in.at[tp], s2.at[i], r2.at[i], {"tp": spot})
        for i, spot in enumerate(tp_spots)
    ]
    for copy in second:
        copy.wait_recv()
    total = tp_in[0]
    for at in range(1, t):
        total = total + tp_in[at]
    out[...] = total
    for copy in first + second:
        copy.wait_send()


def totals_exchange(n, t, x):
    vmem = pl.BlockSpec(memory_space=VMEM)
    rows, lanes = x.shape
    return pl.pallas_call(
        functools.partial(totals_kernel, n, t),
        out_shape=jax.ShapeDtypeStruct((rows, lanes), F32),
        in_specs=[vmem],
        out_specs=vmem,
        scratch_shapes=[
            VMEM((n, rows, lanes), F32),
            VMEM((rows, lanes), F32),
            VMEM((t, rows, lanes), F32),
            DMA((n - 1,)),
            DMA((n - 1,)),
            DMA((t - 1,)),
            DMA((t - 1,)),
            DMA((1,)),
        ],
        compiler_params=pltpu.CompilerParams(collective_id=3, has_side_effects=True),
    )(x)


def squares(along_ref, before_ref, norms):
    rows, width = along_ref.shape
    step = tile_of(rows, 32)

    def body(i, sums):
        at = pl.ds(pl.multiple_of(i * step, step), step)
        along = along_ref[at, :].astype(F32)
        before = before_ref[at, :].astype(F32)
        products = (along * along, along * before, before * before)
        return tuple(
            have + product.reshape(step // 8, 8, width).sum(axis=0)
            for have, product in zip(sums, products)
        )

    zero = jnp.zeros((8, width), F32)
    sums = lax.fori_loop(0, rows // step, body, (zero, zero, zero))
    for kind in range(3):
        norms[kind] += sums[kind]


def dot(one, two):
    return jnp.dot(one, two, preferred_element_type=F32)


def front_kernel(tokens, gate, up, along_gate, along_up, before_gate, before_up, x, before, norms):
    @pl.when(pl.program_id(0) == 0)
    def _():
        norms[...] = jnp.zeros_like(norms)

    rows = tokens[...]
    for kind, ref in enumerate((gate, up, along_gate, along_up)):
        x[kind] = dot(rows, ref[...]).astype(BF16)
    for kind, ref in enumerate((before_gate, before_up)):
        before[kind] = dot(rows, ref[...]).astype(BF16)
    squares(along_gate, before_gate, norms)
    squares(along_up, before_up, norms)


def front_products(tokens, *matrices):
    rows, depth = tokens.shape
    width = matrices[0].shape[1]
    tile = tile_of(width, 512)
    return pl.pallas_call(
        front_kernel,
        grid=(width // tile,),
        out_shape=(
            jax.ShapeDtypeStruct((4, rows, width), BF16),
            jax.ShapeDtypeStruct((2, rows, width), BF16),
            jax.ShapeDtypeStruct((3, 8, tile), F32),
        ),
        in_specs=[pl.BlockSpec((rows, depth), lambda i: (0, 0))]
        + [pl.BlockSpec((depth, tile), lambda i: (0, i))] * 6,
        out_specs=(
            pl.BlockSpec((4, rows, tile), lambda i: (0, 0, i)),
            pl.BlockSpec((2, rows, tile), lambda i: (0, 0, i)),
            pl.BlockSpec((3, 8, tile), lambda i: (0, 0, 0)),
        ),
        compiler_params=pltpu.CompilerParams(vmem_limit_bytes=LIMIT),
    )(tokens, *matrices)


def middle_kernel(units, down, along, before, weighted, moved, was, norms):
    @pl.when(pl.program_id(0) == 0)
    def _():
        for ref in (weighted, moved, was, norms):
            ref[...] = jnp.zeros_like(ref)

    rows = units[...]
    weighted[...] += dot(rows, down[...])
    moved[...] += dot(rows, along[...])
    was[...] += dot(rows, before[...])
    squares(along, before, norms)


def middle_products(units, down, along, before):
    rows, depth = units.shape
    width = down.shape[1]
    tile = tile_of(depth, 512)
    whole = pl.BlockSpec((rows, width), lambda i: (0, 0))
    return pl.pallas_call(
        middle_kernel,
        grid=(depth // tile,),
        out_shape=[jax.ShapeDtypeStruct((rows, width), F32)] * 3
        + [jax.ShapeDtypeStruct((3, 8, width), F32)],
        in_specs=[pl.BlockSpec((rows, tile), lambda i: (0, i))]
        + [pl.BlockSpec((tile, width), lambda i: (i, 0))] * 3,
        out_specs=[whole] * 3 + [pl.BlockSpec((3, 8, width), lambda i: (0, 0, 0))],
        compiler_params=pltpu.CompilerParams(vmem_limit_bytes=LIMIT),
    )(units, down, along, before)


def against(one, two):
    return lax.dot_general(one, two, (((1,), (1,)), ((), ())), preferred_element_type=F32)


def transposed(one, two):
    return lax.dot_general(one, two, (((0,), (0,)), ((), ())), preferred_element_type=F32)


def back_kernel(grads, down, along, x):
    rows = grads.shape[0] // 2
    weighted = against(grads[...], down[...])
    moved = against(grads[:rows, :], along[...])
    x[0] = weighted[:rows].astype(BF16)
    x[1] = (weighted[rows:] + moved).astype(BF16)


def back_products(grads, down, along):
    rows, depth = grads.shape
    width = down.shape[0]
    tile = tile_of(width, 512)
    return pl.pallas_call(
        back_kernel,
        grid=(width // tile,),
        out_shape=jax.ShapeDtypeStruct((2, rows // 2, width), BF16),
        in_specs=[pl.BlockSpec((rows, depth), lambda i: (0, 0))]
        + [pl.BlockSpec((tile, depth), lambda i: (i, 0))] * 2,
        out_specs=pl.BlockSpec((2, rows // 2, tile), lambda i: (0, 0, i)),
        compiler_params=pltpu.CompilerParams(vmem_limit_bytes=LIMIT),
    )(grads, down, along)


def next_kernel(count, scales, *refs):
    one, rest = refs[0], refs[1:]
    twos, alongs, befores, outs = (rest[i * count : (i + 1) * count] for i in range(4))
    inverse, alpha, beta = scales[0], scales[1], scales[2]
    for two, along, before, out in zip(twos, alongs, befores, outs):
        image = transposed(one[...], two[...])
        out[...] = (
            image * inverse - along[...].astype(F32) * alpha - before[...].astype(F32) * beta
        ).astype(BF16)


def next_parts(scales, one, twos, alongs, befores):
    count = len(twos)
    rows, height = one.shape
    width = twos[0].shape[1]
    tile = tile_of(height, max(128, (1 << 20) // (width * count)))
    block = pl.BlockSpec((tile, width), lambda i: (i, 0))
    return pl.pallas_call(
        functools.partial(next_kernel, count),
        grid=(height // tile,),
        out_shape=[jax.ShapeDtypeStruct((height, width), BF16)] * count,
        in_specs=[pl.BlockSpec(memory_space=pltpu.SMEM), pl.BlockSpec((rows, tile), lambda i: (0, i))]
        + [pl.BlockSpec((rows, width), lambda i: (0, 0))] * count
        + [block] * (2 * count),
        out_specs=[block] * count,
        compiler_params=pltpu.CompilerParams(vmem_limit_bytes=LIMIT),
    )(scales, one, *twos, *alongs, *befores)


def on_device(
    n,
    t,
    tokens,
    targets,
    gate_weight,
    up_weight,
    down_weight,
    direction_gate,
    direction_up,
    direction_down,
    previous_gate,
    previous_up,
    previous_down,
    beta_prev,
):
    everyone = tokens_exchange(t, tokens)
    rows = everyone.shape[0]
    x, before, norms = front_products(
        everyone, gate_weight, up_weight, direction_gate, direction_up, previous_gate, previous_up
    )
    units, keeps = width_exchange(n, x, None, forward_rows, 4)
    units = units.reshape(2 * rows, -1)
    weighted, moved, was, down_norms = middle_products(
        units, down_weight, direction_down, previous_down
    )
    outputs = jnp.stack([weighted[:rows], weighted[rows:] + moved[:rows]]).astype(BF16)
    grads = output_exchange(t, outputs, targets)
    grads = grads.reshape(2 * rows, -1)
    y = back_products(grads, down_weight, direction_down)
    dirs, _ = width_exchange(n, y, keeps, backward_rows, 5)

    swapped = jnp.concatenate([units[rows:], units[:rows]])
    gram = against(dirs[0], dirs[0]) + against(dirs[1], dirs[1])
    image_image = jnp.sum(against(everyone, everyone) * gram) + jnp.sum(
        against(swapped, swapped) * against(grads, grads)
    )
    swapped_moved = jnp.concatenate([moved[rows:], moved[:rows]])
    swapped_was = jnp.concatenate([was[rows:], was[:rows]])
    wide = dirs.astype(F32)
    tall = grads.astype(F32)
    image_along = jnp.sum(wide * x[2:].astype(F32)) + jnp.sum(tall * swapped_moved)
    image_before = jnp.sum(wide * before.astype(F32)) + jnp.sum(tall * swapped_was)
    own = jnp.sum(norms, axis=(1, 2)) + jnp.sum(down_norms, axis=(1, 2))
    sums = jnp.concatenate([jnp.stack([image_image, image_along, image_before]), own])
    sums = jnp.broadcast_to(jnp.pad(sums, (0, 2))[:, None], (8, 128))
    totals = totals_exchange(n, t, sums)[:, 0]
    image_image, image_along, image_before = totals[0], totals[1], totals[2]
    along_along, along_before, before_before = totals[3], totals[4], totals[5]
    entries = float(
        n * t * (gate_weight.size + up_weight.size + down_weight.size)
    )
    beta_old = beta_prev[0]
    alpha_coef = image_along / entries
    square = (
        image_image
        - 2.0 * alpha_coef * image_along
        - 2.0 * beta_old * image_before
        + alpha_coef * alpha_coef * along_along
        + 2.0 * alpha_coef * beta_old * along_before
        + beta_old * beta_old * before_before
    )
    beta_coef = jnp.sqrt(square / entries + 1e-06)
    inverse = 1.0 / beta_coef
    scales = jnp.stack([inverse, alpha_coef * inverse, beta_old * inverse])
    next_gate, next_up = next_parts(
        scales,
        everyone,
        (dirs[0], dirs[1]),
        (direction_gate, direction_up),
        (previous_gate, previous_up),
    )
    (next_down,) = next_parts(scales, swapped, (grads,), (direction_down,), (previous_down,))
    return (next_gate, next_up, next_down, jnp.stack([alpha_coef, beta_coef]))


def solution(mesh):
    wide, tall = P("dp", "tp"), P("tp", "dp")
    in_specs = (tall, tall, wide, wide, tall, wide, wide, tall, wide, wide, tall, P())
    return jax.shard_map(
        functools.partial(on_device, mesh.shape["dp"], mesh.shape["tp"]),
        mesh=mesh,
        in_specs=in_specs,
        out_specs=(wide, wide, tall, P()),
        check_vma=False,
    )
```

time: 508 us -> 261 us (0.51)
  Pallas kernels: 0 us -> 223 us
  waiting for transfers between devices: 155 us -> 0 us
  matrix products: 101 us -> 5.6 us
  blocking collectives: 83.9 us -> 0 us
  local copies, waits for them, and re-layouts: 75.3 us -> 6.12 us
  other arithmetic: 57.3 us -> 13.8 us
  between operations: 32.3 us -> 11.8 us
    pallas_call x0 -> x10, Pallas kernels: none -> 223 us  [the longest x2 81.6 us: width_exchange(): pl.pallas_call(functools.partial(width_kernel, n, kinds, rows_of, keeps_i...]
    reduce_scatter x3 -> x0, waiting for transfers between devices: 101 us -> none  [the longest x1 73.1 us: on_device(): lax.psum_scatter(jnp.concatenate([product(everyone, gate_weight), product...]
    dot_general x14 -> x5, matrix products: 101 us -> 5.6 us  [against(): lax.dot_general(one, two, (((1,), (1,)), ((), ())), preferred_element_typ...]
    unnamed x26 -> x8, local copies, waits for them, and re-layouts: 75.3 us -> 0.98 us
    all_gather x4 -> x0, waiting for transfers between devices: 53.9 us -> none  [the longest x1 23 us: on_device(): lax.all_gather(hidden_dir, 'dp', axis=0, tiled=True)]
    convert_element_type x6 -> x0, other arithmetic: 50.5 us -> none  [the longest x2 44.4 us: on_device(): (matrix / beta_coef).astype(jnp.bfloat16)]
    all_gather x3 -> x0, blocking collectives: 44.3 us -> none  [the longest x1 16 us: on_device(): everyone = lax.all_gather(tokens, 'tp', axis=0, tiled=True)]
    psum x1 -> x0, blocking collectives: 39.6 us -> none  [on_device(): lax.psum((inner_sum(images, images), inner_sum(images, alongs), inner_sum...]
  transfers between devices with their start and end apart: 7 -> 0, of which waited for: 6 -> 0; matrix products, arithmetic and copies ran while one was open for 19% -> 0% of each run, Pallas kernels for 0% -> 0%
where the time goes in v1:
time: 261 us; the launch traced here: 260 us
  Pallas kernels  223 us (85%)
  other arithmetic  13.8 us (5%)
  between operations  11.8 us (5%)
  local copies, waits for them, and re-layouts  6.12 us (2%)
  matrix products  5.6 us (2%)
    pallas_call x2, Pallas kernels, width_exchange(): pl.pallas_call(functools.partial(width_kernel, n, kinds, rows_of, keeps_i...  81.6 us
    pallas_call x2, Pallas kernels, next_parts(): pl.pallas_call(functools.partial(next_kernel, count), grid=(height // til...  33.7 us
    pallas_call x1, Pallas kernels, output_exchange(): pl.pallas_call(functools.partial(output_kernel, t), out_shape=jax.ShapeDt...  26.9 us
    pallas_call x1, Pallas kernels, front_products(): pl.pallas_call(front_kernel, grid=(width // tile,), out_shape=(jax.ShapeD...  25.2 us
    pallas_call x1, Pallas kernels, middle_products(): pl.pallas_call(middle_kernel, grid=(depth // tile,), out_shape=[jax.Shape...  17.4 us
    pallas_call x1, Pallas kernels, totals_exchange(): pl.pallas_call(functools.partial(totals_kernel, n, t), out_shape=jax.Shap...  14.5 us
    pallas_call x1, Pallas kernels, tokens_exchange(): pl.pallas_call(functools.partial(tokens_kernel, t), out_shape=jax.ShapeDt...  11.8 us
    pallas_call x1, Pallas kernels, back_products(): pl.pallas_call(back_kernel, grid=(width // tile,), out_shape=jax.ShapeDty...  11.6 us

profile of v1, /device:TPU:0, one launch (start us, length us, event | category | flops | bytes accessed | tf_op | source)
XLA Modules:
  0.0 260.2 jit_solution(5223125886932863699)
XLA Ops:
  1.3 11.8 %shard_map.147 = bf16[4,32,1024]{2,1,0:T(8,128)(2,1)} custom-call(bf16[32,1024]{1,0:T(8,128)(2,1)} %x.3), custom_call_target="tpu_custom_call" | custom-call | tf_op jit(solution)/shard_map/pallas_call | solution.py:208
  13.1 1.3 fusion.13
  14.4 25.2 %shard_map.148 = (bf16[4,128,4096]{2,1,0:T(8,128)(2,1)}, bf16[2,128,4096]{2,1,0:T(8,128)(2,1)}, f32[3,8,512]{2,1,0:T(8,128)}) custom-call(bf16[128,1024]{1,0:T(8,128)(2,1)} %bitcast.56, bf16[1024,4096]{1,0:T(8,128)(2,1)} %gate.1, bf16[1024,4096]{1,0:T(8,128)(2,1)} %up.1, bf16[1024,4096]{1,0:T(8,128)(2,1)} %refs_3_.2, bf16[1024,4096]{1,0:T(8,128)(2,1)} %refs_4_.1, ...), custom_call_target="tpu_custom_call" | custom-call | tf_op jit(solution)/shard_map/pallas_call | solution.py:374
  39.6 0.9 reduce_sum.78
  40.5 47.4 %shard_map.149 = (bf16[2,8,16,4096]{3,2,1,0:T(8,128)(2,1)}, f32[16,4096]{1,0:T(8,128)}, f32[16,4096]{1,0:T(8,128)}, f32[16,4096]{1,0:T(8,128)}, f32[16,4096]{1,0:T(8,128)}) custom-call(bf16[4,4,2,16,4096]{4,3,2,1,0:T(8,128)(2,1)} %bitcast.52), custom_call_target="tpu_custom_call" | custom-call | tf_op jit(solution)/shard_map/pallas_call | solution.py:167
  88.0 1.8 fusion.8
  89.7 0.7 fusion.7
  90.5 1.6 pad_maximum_fusion.refs_0_
  92.0 17.4 %shard_map.150 = (f32[256,1024]{1,0:T(8,128)}, f32[256,1024]{1,0:T(8,128)}, f32[256,1024]{1,0:T(8,128)}, f32[3,8,1024]{2,1,0:T(8,128)}) custom-call(bf16[256,4096]{1,0:T(8,128)(2,1)} %bitcast.54, bf16[4096,1024]{1,0:T(8,128)(2,1)} %down.3, bf16[4096,1024]{1,0:T(8,128)(2,1)} %refs_2_.1, bf16[4096,1024]{1,0:T(8,128)(2,1)} %refs_3_.3), custom_call_target="tpu_custom_call" | custom-call | tf_op jit(solution)/shard_map/pallas_call | solution.py:411
  109.4 1.0 reduce_sum.79
  110.4 1.1 slice.102
  111.5 2.0 fusion.10
  113.5 0.1 pad_maximum_fusion.2
  113.6 0.8 pad_maximum_fusion.3.x
  114.5 26.9 %shard_map.151 = bf16[2,4,32,1024]{3,2,1,0:T(8,128)(2,1)} custom-call(bf16[2,4,32,1024]{3,2,1,0:T(8,128)(2,1)} %pad_maximum_fusion.3.x, bf16[32,1024]{1,0:T(8,128)(2,1)} %targets.1), custom_call_target="tpu_custom_call" | custom-call | tf_op jit(solution)/shard_map/pallas_call | solution.py:267
  141.4 2.1 fusion.5
  143.5 0.1 pad_maximum_fusion.1
  143.6 2.0 fusion.3
  145.6 11.6 %shard_map.152 = bf16[2,128,4096]{2,1,0:T(8,128)(2,1)} custom-call(bf16[256,1024]{1,0:T(8,128)(2,1)} %bitcast.46, bf16[4096,1024]{1,0:T(8,128)(2,1)} %down.3, bf16[4096,1024]{1,0:T(8,128)(2,1)} %refs_2_.1), custom_call_target="tpu_custom_call" | custom-call | tf_op jit(solution)/shard_map/pallas_call | solution.py:443
  157.2 34.2 %shard_map.153 = bf16[2,8,16,4096]{3,2,1,0:T(8,128)(2,1)} custom-call(bf16[2,4,2,16,4096]{4,3,2,1,0:T(8,128)(2,1)} %bitcast.53, f32[16,4096]{1,0:T(8,128)} %get-tuple-element.22.refs_1_, f32[16,4096]{1,0:T(8,128)} %get-tuple-element.23.refs_2_, f32[16,4096]{1,0:T(8,128)} %get-tuple-element.24.refs_3_, f32[16,4096]{1,0:T(8,128)} %get-tuple-element.25.refs_4_), custom_call_target="tpu_custom_call" | custom-call | tf_op jit(solution)/shard_map/pallas_call | solution.py:167
  191.4 4.1 %fusion = (f32[]{:T(128)}, f32[]{:T(128)}) fusion(bf16[2,8,16,4096]{3,2,1,0:T(8,128)(2,1)} %shard_map.153, bf16[4,128,4096]{2,1,0:T(8,128)(2,1)S(1)} %copy-done.3, bf16[2,128,4096]{2,1,0:T(8,128)(2,1)} %get-tuple-element.26), kind=kLoop, calls=%fused_computation.2 | loop fusion | flops 7340030 | bytes 6291464 | tf_op jit(solution)/shard_map/reduce_sum | solution.py:524
  198.1 0.2 fusion.9
  198.3 1.0 copy-done.2
  199.3 0.4 fusion.14
  199.7 1.0 fusion.6
  202.0 0.7 broadcast_in_dim.2.x
  202.7 14.5 %shard_map.154 = f32[8,128]{1,0:T(8,128)} custom-call(f32[8,128]{1,0:T(8,128)} %broadcast_in_dim.2.x), custom_call_target="tpu_custom_call" | custom-call | tf_op jit(solution)/shard_map/pallas_call | solution.py:313
  217.2 1.5 fusion.12
  225.3 0.6 pad_maximum_fusion.4.scales
  225.8 0.6 pad_maximum_fusion.5
  226.4 12.2 %shard_map.156 = bf16[4096,1024]{1,0:T(8,128)(2,1)} custom-call(f32[3]{0:T(128)} %pad_maximum_fusion.4.scales, bf16[256,4096]{1,0:T(8,128)(2,1)} %pad_maximum_fusion.refs_0_, bf16[256,1024]{1,0:T(8,128)(2,1)} %bitcast.47, bf16[4096,1024]{1,0:T(8,128)(2,1)} %refs_2_.1, bf16[4096,1024]{1,0:T(8,128)(2,1)} %refs_3_.3), custom_call_target="tpu_custom_call" | custom-call | tf_op jit(solution)/shard_map/pallas_call | solution.py:471
  238.6 21.6 %shard_map.155 = (bf16[1024,4096]{1,0:T(8,128)(2,1)}, bf16[1024,4096]{1,0:T(8,128)(2,1)}) custom-call(f32[3]{0:T(128)} %pad_maximum_fusion.4.scales, bf16[128,1024]{1,0:T(8,128)(2,1)} %bitcast.57, bf16[128,4096]{1,0:T(8,128)(2,1)} %bitcast.51, bf16[128,4096]{1,0:T(8,128)(2,1)} %bitcast.49, bf16[1024,4096]{1,0:T(8,128)(2,1)} %refs_3_.2, ...), custom_call_target="tpu_custom_call" | custom-call | tf_op jit(solution)/shard_map/pallas_call | solution.py:471
  (9 shorter events, 0.1 us)
Async XLA Ops:
  157.2 34.2 %copy-start.3 = (bf16[4,128,4096]{2,1,0:T(8,128)(2,1)S(1)}, bf16[4,128,4096]{2,1,0:T(8,128)(2,1)}, u32[]{:S(2)}) copy-start(bf16[4,128,4096]{2,1,0:T(8,128)(2,1)} %get-tuple-element.18) | copy-start | bytes 12582916
  191.4 6.7 %copy-start = (bf16[2,8,16,4096]{3,2,1,0:T(8,128)(2,1)S(1)}, bf16[2,8,16,4096]{3,2,1,0:T(8,128)(2,1)}, u32[]{:S(2)}) copy-start(bf16[2,8,16,4096]{3,2,1,0:T(8,128)(2,1)} %shard_map.153) | copy-start | bytes 6291460
  198.3 1.0 copy-start.2
  198.3 40.3 %copy-start.1 = (bf16[1,8,16,4096]{3,2,1,0:T(8,128)(2,1)}, bf16[1,8,16,4096]{3,2,1,0:T(8,128)(2,1)S(1)}, u32[]{:S(2)}) copy-start(bf16[1,8,16,4096]{3,2,1,0:T(8,128)(2,1)S(1)} %get-tuple-element.38) | copy-start | bytes 3145732
